TPU v7x, 32 devices: a whole 2x2x4 slice. The times are simulated.
32 devices in a mesh: grp: 2 (over y), tp: 8 (over z, x), sub: 2 (over core).
Axes of the slice: x: 2, y: 2, z: 4, core: 2. Of those that a mesh axis runs over, the one named last changes fastest.
Arguments:
- hidden_in: bfloat16 [32, 2, 4096], P('grp', 'sub', 'tp'), parts along dimension 0, may hold values from -16 to 16
- norm_attn: float32 [8192], replicated, may hold values from 0.25 to 1.75
- w_query: bfloat16 [8192, 2, 4096], P(None, 'sub', 'tp'), may hold values from -0.0625 to 0.0625
- w_key: bfloat16 [8192, 2, 512], P(None, 'sub', 'tp'), may hold values from -0.0625 to 0.0625
- w_value: bfloat16 [8192, 2, 512], P(None, 'sub', 'tp'), may hold values from -0.0625 to 0.0625
- w_out: bfloat16 [2, 4096, 2, 4096], P('sub', None, None, 'tp'), may hold values from -0.0625 to 0.0625
- norm_ffn: float32 [8192], replicated, may hold values from 0.25 to 1.75
- w_gate: bfloat16 [2, 4096, 14336], P('sub', None, 'tp'), may hold values from -0.0625 to 0.0625
- w_up: bfloat16 [2, 4096, 14336], P('sub', None, 'tp'), may hold values from -0.0625 to 0.0625
- w_down: bfloat16 [14336, 2, 4096], P('tp', 'sub'), may hold values from -0.0625 to 0.0625
- cache_keys: bfloat16 [32, 64, 8, 128], P('grp', 'tp', 'sub'), parts along dimension 0, may hold values from -250 to 250
- cache_values: bfloat16 [32, 64, 8, 128], P('grp', 'tp', 'sub'), parts along dimension 0, may hold values from -6 to 6
- lengths: int32 [32], P('grp'), parts along dimension 0, may hold values from 1 to 64, as said below
Outputs:
- hidden_out: bfloat16 [32, 2, 4096], P('grp', 'sub', 'tp'), parts along dimension 0
There are 2 independent parts, one for each index of `grp`. A program takes and returns all parts, laid end to end along the dimension named above; an argument that names none is the same for every part. Nothing has to cross between parts.
Inputs may be any that keep to these rules, and one draw needn't show every extreme that they name: `lengths`: some sequence has 64 live positions and some has 1.
All inputs are finite; a program needn't handle non-finite values.
Results may differ from a plain program's by a relative error of at most 0.012.
The roundings to bfloat16 on the way count: a program that leaves them out, or rounds other values in their place, can miss the bound.
Values may be sent and summed in bfloat16 or wider, within the bound.
A program may use at most 128 MiB of HBM per device.

v0:
```python
import math
import jax
import jax.numpy as jnp
from jax import lax
from jax.sharding import PartitionSpec as P

HD = 128
epsilon = 1e-05
rope_base = 500000.0
floor_score = -1e30


def joined(part, axis, combine):
    gathered = jax.tree.map(lambda a: lax.all_gather(a, axis), part)

    def take(source):
        return jax.tree.map(lambda a: lax.dynamic_index_in_dim(a, source, 0, False), gathered)

    return lax.fori_loop(
        1, lax.axis_size(axis), lambda source, state: combine(state, take(source)), take(0)
    )


def rope_angles(lengths):
    frequencies = rope_base ** (-(jnp.arange(HD // 2, dtype=jnp.float32) * 2.0) / HD)
    return lengths.astype(jnp.float32)[:, None] * frequencies[None, :]


def rotate(vectors, angles):
    middle_index = vectors.shape[-1] // 2
    cosine = jnp.cos(angles)[:, None, :]
    sine = jnp.sin(angles)[:, None, :]
    lower = vectors[..., :middle_index]
    upper = vectors[..., middle_index:]
    return jnp.concatenate([lower * cosine - upper * sine, upper * cosine + lower * sine], axis=-1)


def spread_rows(shard):
    across = lax.all_gather(shard, "tp", axis=2, tiled=True)
    return lax.all_gather(across, "sub", axis=1, tiled=True)


def half_rows_of(shard):
    return lax.all_gather(shard, "tp", axis=2, tiled=True)


def join_partials(earlier, later):
    earlier_max, earlier_sum, earlier_out = earlier
    later_max, later_sum, later_out = later
    highest = jnp.maximum(earlier_max, later_max)
    earlier_scale = jnp.exp(earlier_max - highest)
    later_scale = jnp.exp(later_max - highest)
    joined_sum = earlier_sum * earlier_scale + later_sum * later_scale
    joined_out = earlier_out * earlier_scale[..., None] + later_out * later_scale[..., None]
    return (highest, joined_sum, joined_out)


def per_device(
    hidden_in,
    norm_attn,
    w_query,
    w_key,
    w_value,
    w_out,
    norm_ffn,
    w_gate,
    w_up,
    w_down,
    cache_keys,
    cache_values,
    lengths,
):
    seq_count = hidden_in.shape[0]
    shard_width = hidden_in.shape[2]
    half_width = shard_width * lax.axis_size("tp")
    model_width = half_width * lax.axis_size("sub")
    tp_pos = lax.axis_index("tp")
    sub_pos = lax.axis_index("sub")
    residual = hidden_in.astype(jnp.float32)
    whole_rows = spread_rows(hidden_in).astype(jnp.float32)
    factor = lax.rsqrt(jnp.mean(whole_rows * whole_rows, axis=(1, 2)) + epsilon)
    gain_whole = norm_attn.reshape(whole_rows.shape[1], half_width)
    gathered = (whole_rows * factor[:, None, None] * gain_whole).astype(jnp.bfloat16)
    flattened = gathered.reshape(seq_count, model_width)
    query_part = jnp.dot(
        flattened, w_query.reshape(model_width, -1), preferred_element_type=jnp.float32
    ).astype(jnp.bfloat16)
    key_part = jnp.dot(
        flattened, w_key.reshape(model_width, -1), preferred_element_type=jnp.float32
    ).astype(jnp.bfloat16)
    value_part = jnp.dot(
        flattened, w_value.reshape(model_width, -1), preferred_element_type=jnp.float32
    ).astype(jnp.bfloat16)
    query, key_new, value_new = (
        lax.all_gather(query_part, "tp", axis=1, tiled=True),
        lax.all_gather(key_part, "tp", axis=1, tiled=True),
        lax.all_gather(value_part, "tp", axis=1, tiled=True),
    )
    query_heads = query.shape[1] // HD
    kv_heads = key_new.shape[1] // HD
    group_size = query_heads // kv_heads
    angles = rope_angles(lengths)
    query_rot = rotate(
        query.astype(jnp.float32).reshape(seq_count, query_heads, HD), angles
    ).astype(jnp.bfloat16)
    key_rot = rotate(key_new.astype(jnp.float32).reshape(seq_count, kv_heads, HD), angles).astype(
        jnp.bfloat16
    )
    grouped = query_rot.reshape(seq_count, kv_heads, group_size, HD)
    values_new = value_new.astype(jnp.float32).reshape(seq_count, kv_heads, 1, HD)
    span = cache_keys.shape[1]
    scores = jnp.einsum(
        "bkgd,blkd->bkgl", grouped, cache_keys, preferred_element_type=jnp.float32
    ) / math.sqrt(HD)
    places = tp_pos * span + jnp.arange(span, dtype=jnp.int32)
    live = (places[None, :] < lengths[:, None])[:, None, None, :]
    masked = jnp.where(live, scores, floor_score)
    local_max = jnp.max(masked, axis=-1)
    weights = jnp.where(live, jnp.exp(masked - local_max[..., None]), 0.0)
    local_sum = jnp.sum(weights, axis=-1)
    local_out = jnp.einsum(
        "bkgl,blkd->bkgd",
        weights,
        cache_values.astype(jnp.float32),
        precision=lax.Precision.HIGHEST,
    )
    own_score = jnp.sum(
        grouped.astype(jnp.float32) * key_rot.astype(jnp.float32)[:, :, None, :], axis=-1
    ) / math.sqrt(HD)
    joined_max, joined_sum, joined_out = joined(
        (local_max, local_sum, local_out), "tp", join_partials
    )
    highest = jnp.maximum(joined_max, own_score)
    kept_scale = jnp.exp(joined_max - highest)
    own_weight = jnp.exp(own_score - highest)
    numerator = joined_out * kept_scale[..., None] + own_weight[..., None] * values_new
    denominator = joined_sum * kept_scale + own_weight
    attended = (numerator / denominator[..., None]).reshape(seq_count, -1).astype(jnp.bfloat16)
    out_part = jnp.dot(
        attended, w_out.reshape(attended.shape[1], -1), preferred_element_type=jnp.float32
    )
    out_part = out_part.reshape(seq_count, -1, shard_width)
    mixed = lax.psum_scatter(out_part, "sub", scatter_dimension=1, tiled=True)
    middle = (residual + mixed).astype(jnp.bfloat16)
    middle_float = middle.astype(jnp.float32)
    raw_half = half_rows_of(middle).astype(jnp.float32)
    partial_squares = jnp.sum(raw_half * raw_half, axis=(1, 2))
    squares_mid = lax.psum(partial_squares, "sub")
    factor_mid = lax.rsqrt(squares_mid / model_width + epsilon)
    gain_half = lax.dynamic_slice_in_dim(norm_ffn, sub_pos * half_width, half_width)
    half_rows = (raw_half * factor_mid[:, None, None] * gain_half).astype(jnp.bfloat16)
    half_flat = half_rows.reshape(seq_count, half_width)
    gate_part = jnp.dot(
        half_flat, w_gate.reshape(half_width, -1), preferred_element_type=jnp.float32
    )
    up_part = jnp.dot(half_flat, w_up.reshape(half_width, -1), preferred_element_type=jnp.float32)
    gate_total, up_total = lax.psum((gate_part, up_part), "sub")
    hidden = (jax.nn.silu(gate_total) * up_total).astype(jnp.bfloat16)
    down_part = jnp.dot(
        hidden, w_down.reshape(hidden.shape[1], -1), preferred_element_type=jnp.float32
    )
    down_total = lax.psum(down_part, "tp")
    down_share = lax.dynamic_slice_in_dim(down_total, tp_pos * shard_width, shard_width, 1)
    return (middle_float + down_share[:, None, :]).astype(jnp.bfloat16)


def solution(mesh):
    in_specs = (
        P("grp", "sub", "tp"),
        P(),
        P(None, "sub", "tp"),
        P(None, "sub", "tp"),
        P(None, "sub", "tp"),
        P("sub", None, None, "tp"),
        P(),
        P("sub", None, "tp"),
        P("sub", None, "tp"),
        P("tp", "sub", None),
        P("grp", "tp", "sub", None),
        P("grp", "tp", "sub", None),
        P("grp"),
    )
    out_specs = P("grp", "sub", "tp")
    return jax.shard_map(
        per_device, mesh=mesh, in_specs=in_specs, out_specs=out_specs, check_vma=False
    )
```

profile of v0, /device:TPU:0, one launch (start us, length us, event | category | flops | bytes accessed | tf_op | source)
XLA Modules:
  0.0 410.7 jit_solution(6426538400944346462)
XLA Ops:
  6.6 32.7 %all_gather.36 = bf16[16,1,4096]{2,0,1:T(8,128)(2,1)S(1)} all-gather(bf16[16,1,512]{2,0,1:T(8,128)(2,1)} %param.15), channel_id=1, replica_groups=mesh['grp'=2,'tp'=8,'sub'=2] {'tp'}, dimensions={2}, use_global_device_ids=true | all-gather | bytes 147456 | tf_op jit(solution)/shard_map/all_gather | solution.py:39
  39.3 2.0 all_gather.37
  41.3 0.2 fusion.19
  41.5 0.8 mul.255
  42.3 0.1 fusion.25
  42.4 4.6 %fusion.12 = bf16[16,512]{1,0:T(8,128)(2,1)S(1)} fusion(bf16[16,8192]{1,0:T(8,128)(2,1)S(1)} %bitcast.90, bf16[8192,1,512]{2,0,1:T(8,128)(2,1)} %param.17), kind=kOutput, calls=%fused_computation.18 | convolution fusion | flops 134225920 | bytes 8667136 | tf_op jit(solution)/shard_map/dot_general | solution.py:85
  47.0 30.5 %all_gather.38 = bf16[16,4096]{1,0:T(8,128)(2,1)S(1)} all-gather(bf16[16,512]{1,0:T(8,128)(2,1)S(1)} %fusion.12), channel_id=1, replica_groups=mesh['grp'=2,'tp'=8,'sub'=2] {'tp'}, dimensions={1}, use_global_device_ids=true | all-gather | bytes 147456 | tf_op jit(solution)/shard_map/all_gather | solution.py:95
  77.7 0.1 multiply_cosine_fusion
  77.8 0.1 fusion.28
  78.0 0.3 fusion.48
  78.3 1.3 fusion.26
  79.7 0.2 fusion.27
  79.9 31.0 %all-gather.1 = f32[128,4,8]{2,1,0:T(4,128)S(1)} all-gather(f32[16,4,8]{2,1,0:T(4,128)S(1)} %fusion.27), channel_id=3, replica_groups=mesh['grp'=2,'tp'=8,'sub'=2] {'tp'}, dimensions={0}, use_global_device_ids=true | all-gather | bytes 18432 | tf_op jit(solution)/shard_map/all_gather | solution.py:14
  110.9 0.1 copy.68
  111.0 0.1 copy.66
  111.1 31.7 %all-gather = f32[128,4,8]{2,1,0:T(4,128)S(1)} all-gather(f32[16,4,8]{2,1,0:T(4,128)S(1)} %get-tuple-element.236), channel_id=2, replica_groups=mesh['grp'=2,'tp'=8,'sub'=2] {'tp'}, dimensions={0}, use_global_device_ids=true | all-gather | bytes 18432 | tf_op jit(solution)/shard_map/all_gather | solution.py:14
  142.8 0.1 copy.67
  142.9 0.1 copy.65
  143.0 0.4 fusion.15
  143.4 30.6 %all-gather.3 = bf16[8,64,16]{1,2,0:T(8,128)(2,1)S(1)} all-gather(bf16[1,64,16]{1,2,0:T(8,128)(2,1)S(1)} %fusion.15), channel_id=1, replica_groups=mesh['grp'=2,'tp'=8,'sub'=2] {'tp'}, dimensions={0}, use_global_device_ids=true | all-gather | bytes 18432 | tf_op jit(solution)/shard_map/all_gather | solution.py:96
  174.2 0.1 subtract_convert_fusion.1
  174.3 0.3 multiply_reduce_fusion
  174.7 0.4 fusion.16
  175.1 30.6 %all-gather.4 = bf16[8,64,16]{1,2,0:T(8,128)(2,1)S(1)} all-gather(bf16[1,64,16]{1,2,0:T(8,128)(2,1)S(1)} %fusion.16), channel_id=1, replica_groups=mesh['grp'=2,'tp'=8,'sub'=2] {'tp'}, dimensions={0}, use_global_device_ids=true | all-gather | bytes 18432 | tf_op jit(solution)/shard_map/all_gather | solution.py:97
  205.8 9.3 %copy.83 = bf16[512,8,2,512]{3,1,2,0:T(8,128)(2,1)} copy(bf16[512,8,2,512]{3,2,1,0:T(2,128)(2,1)} %bitcast.89) | data formatting | bytes 16777216
  215.1 11.4 %copy.75 = bf16[1024,4096]{1,0:T(8,128)(2,1)} copy(bf16[1024,4096]{0,1:T(8,128)(2,1)} %bitcast.88) | data formatting | bytes 16777216 | tf_op jit(solution)/shard_map/dot_general | solution.py:139
  226.5 1.0 slice.26
  227.5 10.0 %while.19 = (s32[]{:T(128)}, f32[16,4,8]{0,2,1:T(8,128)S(1)}, f32[16,4,8]{0,2,1:T(8,128)S(1)}, f32[16,4,8,128]{3,2,1,0:T(8,128)S(1)}, f32[8,16,4,8]{1,3,2,0:T(8,...) while((s32[]{:T(128)}, f32[16,4,8]{0,2,1:T(8,128)S(1)}, ...), condition=%wide.region_4.5_spmd, body=%wide.region_3.4_spmd.sunk | while | flops 199685 | bytes 815255 | solution.py:19
  227.7 1.2 fusion.58
  229.1 1.2 fusion.58
  230.5 1.2 fusion.58
  231.9 1.2 fusion.58
  233.4 1.2 fusion.58
  234.8 1.2 fusion.58
  236.2 1.2 fusion.58
  237.7 0.3 divide_convert_fusion
  238.1 6.3 %fusion.49 = f32[16,2,512]{2,0,1:T(8,128)} fusion(bf16[16,4096,1]{1,0,2:T(8,128)(2,1)S(1)} %reshape.198, bf16[2,512,4096]{2,1,0:T(8,128)(2,1)} %bitcast.87), kind=kOutput, calls=%fused_computation.77 | convolution fusion | flops 134217728 | bytes 8585216 | tf_op jit(solution)/shard_map/dot_general | solution.py:139
  244.5 8.5 %reduce-scatter.2.cloned.1.call-done = f32[16,1,512]{2,0,1:T(8,128)} async-done(((f32[16,2,512]{2,0,1:T(8,128)}), f32[16,1,512]{2,0,1:T(8,128)}) %reduce-scatter.2.cloned.1.call-update) | async-done | bytes 32784 | tf_op jit(solution)/shard_map/reduce_scatter | solution.py:143
  253.0 0.8 add_convert_fusion.1
  253.8 30.8 %all_gather.47 = bf16[16,1,4096]{2,0,1:T(8,128)(2,1)S(1)} all-gather(bf16[16,1,512]{2,0,1:T(8,128)(2,1)S(1)} %add_convert_fusion.1), channel_id=1, replica_groups=mesh['grp'=2,'tp'=8,'sub'=2] {'tp'}, dimensions={2}, use_global_device_ids=true | all-gather | bytes 147456 | tf_op jit(solution)/shard_map/all_gather | solution.py:44
  284.5 0.1 fusion.22
  284.7 2.6 psum.28
  287.3 7.9 %fusion.7 = f32[16,1792]{1,0:T(8,128)} fusion(bf16[1,4096,1792]{2,1,0:T(8,128)(2,1)} %param.22, bf16[16,1,4096]{2,0,1:T(8,128)(2,1)S(1)} %all_gather.47, f32[4096]{0:T(1024)S(1)} %dynamic_slice.50, f32[16]{0:T(128)S(1)} %add_rsqrt_fusion), kind=kOutput, calls=%fused_computation.12 | convolution fusion | flops 235143168 | bytes 14942272 | tf_op jit(solution)/shard_map/dot_general | solution.py:153
  295.2 7.9 %fusion.5 = f32[16,1792]{1,0:T(8,128)} fusion(bf16[1,4096,1792]{2,1,0:T(8,128)(2,1)} %param.23, bf16[16,1,4096]{2,0,1:T(8,128)(2,1)S(1)} %all_gather.47, f32[4096]{0:T(1024)S(1)} %dynamic_slice.50, f32[16]{0:T(128)S(1)} %add_rsqrt_fusion), kind=kOutput, calls=%fused_computation.10 | convolution fusion | flops 235143168 | bytes 14942272 | tf_op jit(solution)/shard_map/dot_general | solution.py:156
  303.2 19.1 %all-reduce.6.cloned.1.call-done = (f32[16,1792]{1,0:T(8,128)}, f32[16,1792]{1,0:T(8,128)}) async-done(((f32[16,1792]{1,0:T(8,128)}, f32[16,1792]{1,0:T(8,128)}), (f32[16,1792]{1,0:T(8,128)}, f32[16,1792]{1,0:T(8,128)})) %all-reduce.6.cloned.1.call-update) | async-done | bytes 229392 | tf_op jit(solution)/shard_map/psum | solution.py:157
  322.4 8.0 %fusion.3 = f32[16,4096]{1,0:T(8,128)} fusion(bf16[1792,1,4096]{2,0,1:T(8,128)(2,1)} %param.24, f32[16,1792]{1,0:T(8,128)} %get-tuple-element.221, f32[16,1792]{1,0:T(8,128)} %get-tuple-element.222), kind=kOutput, calls=%fused_computation.8 | convolution fusion | flops 235053056 | bytes 15171584 | tf_op jit(solution)/shard_map/dot_general | solution.py:159
  330.4 72.4 %all-reduce.4.cloned.1.call-done = f32[16,4096]{1,0:T(8,128)} async-done(((f32[16,4096]{1,0:T(8,128)}), f32[16,4096]{1,0:T(8,128)}) %all-reduce.4.cloned.1.call-update) | async-done | bytes 262160 | tf_op jit(solution)/shard_map/psum | solution.py:162
  402.8 1.4 fusion.37
  (71 shorter events, 2.4 us)
Async XLA Ops:
  6.5 136.5 %copy-start = (bf16[8192,1,64]{0,2,1:T(8,128)(2,1)S(1)}, bf16[8192,1,64]{0,2,1:T(8,128)(2,1)}, u32[]{:S(2)}) copy-start(bf16[8192,1,64]{0,2,1:T(8,128)(2,1)} %param.18) | copy-start | bytes 3145732
  6.5 71.1 %copy-start.7 = (s32[16]{0:T(128)S(1)}, s32[16]{0:T(128)}, u32[]{:S(2)}) copy-start(s32[16]{0:T(128)} %param.27) | copy-start | bytes 196
  6.5 71.4 %copy-start.3 = (bf16[16,8,4,128]{3,2,1,0:T(4,128)(2,1)S(1)}, bf16[16,8,4,128]{3,2,1,0:T(4,128)(2,1)}, u32[]{:S(2)}) copy-start(bf16[16,8,4,128]{3,2,1,0:T(4,128)(2,1)} %param.25) | copy-start | bytes 393220
  6.5 71.8 %copy-start.4 = (bf16[16,8,4,128]{3,2,1,0:T(4,128)(2,1)S(1)}, bf16[16,8,4,128]{3,2,1,0:T(4,128)(2,1)}, u32[]{:S(2)}) copy-start(bf16[16,8,4,128]{3,2,1,0:T(4,128)(2,1)} %param.26) | copy-start | bytes 393220
  6.5 168.1 %copy-start.2 = (bf16[8192,1,64]{0,2,1:T(8,128)(2,1)S(1)}, bf16[8192,1,64]{0,2,1:T(8,128)(2,1)}, u32[]{:S(2)}) copy-start(bf16[8192,1,64]{0,2,1:T(8,128)(2,1)} %param.19) | copy-start | bytes 3145732
  6.5 219.9 %all-gather.7.cloned.1.call-start = ((), (), s32[]{:S(2)}) async-start(), calls=%async_computation.3 | async-start | bytes 2359296 | tf_op jit(solution)/shard_map/all_gather | solution.py:14
  79.7 173.3 %reduce-scatter.2.cloned.1.call-start = ((), (), s32[]{:S(2)}) async-start(), calls=%async_computation.1 | async-start | bytes 98304 | tf_op jit(solution)/shard_map/reduce_scatter | solution.py:143
  215.1 29.3 %copy-start.6 = (f32[8192]{0:T(1024)S(1)}, f32[8192]{0:T(1024)}, u32[]{:S(2)}) copy-start(f32[8192]{0:T(1024)} %param.21) | copy-start | bytes 98308
  215.1 37.9 %copy-start.5 = (bf16[16,1,512]{2,0,1:T(8,128)(2,1)S(1)}, bf16[16,1,512]{2,0,1:T(8,128)(2,1)}, u32[]{:S(2)}) copy-start(bf16[16,1,512]{2,0,1:T(8,128)(2,1)} %param.15) | copy-start | bytes 49156
  244.4 78.0 %all-reduce.6.cloned.1.call-start = ((), (), s32[]{:S(2)}) async-start(), calls=%async_computation.4 | async-start | bytes 458752 | tf_op jit(solution)/shard_map/psum | solution.py:157
  295.2 109.0 %copy-start.1 = (bf16[8192,1,64]{0,2,1:T(8,128)(2,1)S(1)}, bf16[8192,1,64]{0,2,1:T(8,128)(2,1)}, u32[]{:S(2)}) copy-start(bf16[8192,1,64]{0,2,1:T(8,128)(2,1)} %param.18) | copy-start | bytes 3145732
  303.2 99.6 %all-reduce.4.cloned.1.call-start = ((), (), s32[]{:S(2)}) async-start(), calls=%async_computation.2 | async-start | bytes 524288 | tf_op jit(solution)/shard_map/psum | solution.py:162
Sparse Core Ops, SparseCore 0:
  79.8 53.2 all-gather.6
  244.5 8.4 reduce-scatter.1
  303.3 19.0 all-reduce.5
  330.5 72.2 all-reduce.3
where the time goes:
time: 412 us; the launch traced here: 411 us
  blocking collectives  223 us (54%)
  waiting for transfers between devices  100 us (24%)
  matrix products  37.1 us (9%)
  local copies, waits for them, and re-layouts  24.6 us (6%)
  between operations  13.3 us (3%)
  other arithmetic  12.6 us (3%)
    psum x1, waiting for transfers between devices, per_device(): down_total = lax.psum(down_part, 'tp')  72.4 us
    all_gather x2, blocking collectives, joined(): gathered = jax.tree.map(lambda a: lax.all_gather(a, axis), part)  62.7 us
    all_gather x1, blocking collectives, spread_rows(): across = lax.all_gather(shard, 'tp', axis=2, tiled=True)  32.7 us
    all_gather x1, blocking collectives, half_rows_of(): return lax.all_gather(shard, 'tp', axis=2, tiled=True)  30.8 us
    all_gather x1, blocking collectives, per_device(): lax.all_gather(key_part, 'tp', axis=1, tiled=True)  30.6 us
    all_gather x1, blocking collectives, per_device(): lax.all_gather(value_part, 'tp', axis=1, tiled=True)  30.6 us
    all_gather x1, blocking collectives, per_device(): lax.all_gather(query_part, 'tp', axis=1, tiled=True)  30.5 us
    psum x1, waiting for transfers between devices, per_device(): gate_total, up_total = lax.psum((gate_part, up_part), 'sub')  19.1 us
  transfers between devices with their start and end apart: 4, of which 3 were waited for; matrix products, arithmetic and copies ran while one was open for 6% of the time, Pallas kernels for 0%

commit v1 on v0

--- a/solution.py
+++ b/solution.py
@@ -36,7 +36,12 @@
 
 
 def spread_rows(shard):
-    across = lax.all_gather(shard, "tp", axis=2, tiled=True)
+    ring = [shard]
+    for hop in range(7):
+        ring.append(lax.ppermute(ring[-1], "tp", [(dev, (dev + 1) % 8) for dev in range(8)]))
+    across = jnp.roll(
+        jnp.concatenate(ring[::-1], axis=2), (lax.axis_index("tp") + 1) * ring[0].shape[2], axis=2
+    )
     return lax.all_gather(across, "sub", axis=1, tiled=True)
 
 

time: 412 us -> 423 us (1.027)
  waiting for transfers between devices: 100 us -> 138 us
  blocking collectives: 223 us -> 189 us
    ppermute x0 -> x7, waiting for transfers between devices: none -> 41.3 us  [spread_rows(): lax.ppermute(ring[-1], 'tp', [(dev, (dev + 1) % 8) for dev in range(8)])]
    all_gather x1 -> x0, blocking collectives: 32.7 us -> none  [spread_rows(): across = lax.all_gather(shard, 'tp', axis=2, tiled=True)]
    unnamed x18 -> x31, local copies, waits for them, and re-layouts: 9.4 us -> 10.3 us
  transfers between devices with their start and end apart: 4 -> 11, of which waited for: 3 -> 10; matrix products, arithmetic and copies ran while one was open for 6% -> 6% of each run, Pallas kernels for 0% -> 0%
where the time goes in v1:
time: 423 us; the launch traced here: 422 us
  blocking collectives  189 us (45%)
  waiting for transfers between devices  138 us (33%)
  matrix products  37.1 us (9%)
  local copies, waits for them, and re-layouts  26.9 us (6%)
  other arithmetic  13.9 us (3%)
  between operations  13.4 us (3%)
    psum x1, waiting for transfers between devices, per_device(): down_total = lax.psum(down_part, 'tp')  72.4 us
    all_gather x2, blocking collectives, joined(): gathered = jax.tree.map(lambda a: lax.all_gather(a, axis), part)  61.6 us
    ppermute x7, waiting for transfers between devices, spread_rows(): lax.ppermute(ring[-1], 'tp', [(dev, (dev + 1) % 8) for dev in range(8)])  41.3 us
    all_gather x1, blocking collectives, per_device(): lax.all_gather(key_part, 'tp', axis=1, tiled=True)  31.1 us
    all_gather x1, blocking collectives, half_rows_of(): return lax.all_gather(shard, 'tp', axis=2, tiled=True)  30.8 us
    all_gather x1, blocking collectives, per_device(): lax.all_gather(value_part, 'tp', axis=1, tiled=True)  30.6 us
    all_gather x1, blocking collectives, per_device(): lax.all_gather(query_part, 'tp', axis=1, tiled=True)  30.6 us
    psum x1, waiting for transfers between devices, per_device(): gate_total, up_total = lax.psum((gate_part, up_part), 'sub')  19.1 us
  transfers between devices with their start and end apart: 11, of which 10 were waited for; matrix products, arithmetic and copies ran while one was open for 6% of the time, Pallas kernels for 0%

profile of v1, /device:TPU:0, one launch (start us, length us, event | category | flops | bytes accessed | tf_op | source)
XLA Modules:
  0.0 421.7 jit_solution(13579102507456587925)
XLA Ops:
  6.5 3.0 collective-permute-start
  9.6 5.0 %collective-permute-done = bf16[16,1,512]{2,0,1:T(8,128)(2,1)S(1)} collective-permute-done((bf16[16,1,512]{2,0,1:T(8,128)(2,1)}, bf16[16,1,512]{2,0,1:T(8,128)(2,1)S(1)}, u32[]{:S(2)}, u32[]{:S(2)}) %collective-permute-start) | collective-permute-done | bytes 16416 | tf_op jit(solution)/shard_map/ppermute | solution.py:41
  14.5 6.4 %collective-permute-done.1 = bf16[16,1,512]{2,0,1:T(8,128)(2,1)S(1)} collective-permute-done((bf16[16,1,512]{2,0,1:T(8,128)(2,1)S(1)}, bf16[16,1,512]{2,0,1:T(8,128)(2,1)S(1)}, u32[]{:S(2)}, u32[]{:S(2)}) %collective-permute-start.1) | collective-permute-done | bytes 16416 | tf_op jit(solution)/shard_map/ppermute | solution.py:41
  21.0 6.4 %collective-permute-done.2 = bf16[16,1,512]{2,0,1:T(8,128)(2,1)S(1)} collective-permute-done((bf16[16,1,512]{2,0,1:T(8,128)(2,1)S(1)}, bf16[16,1,512]{2,0,1:T(8,128)(2,1)S(1)}, u32[]{:S(2)}, u32[]{:S(2)}) %collective-permute-start.2) | collective-permute-done | bytes 16416 | tf_op jit(solution)/shard_map/ppermute | solution.py:41
  27.4 0.7 convert_element_type.70
  28.1 5.8 %collective-permute-done.3 = bf16[16,1,512]{2,0,1:T(8,128)(2,1)S(1)} collective-permute-done((bf16[16,1,512]{2,0,1:T(8,128)(2,1)S(1)}, bf16[16,1,512]{2,0,1:T(8,128)(2,1)S(1)}, u32[]{:S(2)}, u32[]{:S(2)}) %collective-permute-start.3) | collective-permute-done | bytes 16416 | tf_op jit(solution)/shard_map/ppermute | solution.py:41
  34.0 6.3 %collective-permute-done.4 = bf16[16,1,512]{2,0,1:T(8,128)(2,1)S(1)} collective-permute-done((bf16[16,1,512]{2,0,1:T(8,128)(2,1)S(1)}, bf16[16,1,512]{2,0,1:T(8,128)(2,1)S(1)}, u32[]{:S(2)}, u32[]{:S(2)}) %collective-permute-start.4) | collective-permute-done | bytes 16416 | tf_op jit(solution)/shard_map/ppermute | solution.py:41
  40.3 6.4 %collective-permute-done.5 = bf16[16,1,512]{2,0,1:T(8,128)(2,1)S(1)} collective-permute-done((bf16[16,1,512]{2,0,1:T(8,128)(2,1)S(1)}, bf16[16,1,512]{2,0,1:T(8,128)(2,1)S(1)}, u32[]{:S(2)}, u32[]{:S(2)}) %collective-permute-start.5) | collective-permute-done | bytes 16416 | tf_op jit(solution)/shard_map/ppermute | solution.py:41
  46.7 0.7 broadcast_compare_fusion
  47.5 0.8 mul.259
  48.2 4.9 %collective-permute-done.6 = bf16[16,1,512]{2,0,1:T(8,128)(2,1)S(1)} collective-permute-done((bf16[16,1,512]{2,0,1:T(8,128)(2,1)S(1)}, bf16[16,1,512]{2,0,1:T(8,128)(2,1)S(1)}, u32[]{:S(2)}, u32[]{:S(2)}) %collective-permute-start.6) | collective-permute-done | bytes 16416 | tf_op jit(solution)/shard_map/ppermute | solution.py:41
  53.2 0.7 constant_dynamic-update-slice_fusion.8
  54.0 0.7 constant_dynamic-update-slice_fusion
  54.7 2.0 all_gather.33
  57.1 4.6 %fusion.12 = bf16[16,512]{1,0:T(8,128)(2,1)S(1)} fusion(bf16[16,8192]{1,0:T(8,128)(2,1)S(1)} %bitcast.90, bf16[8192,1,512]{2,0,1:T(8,128)(2,1)} %param.17), kind=kOutput, calls=%fused_computation.18 | convolution fusion | flops 134225920 | bytes 8667136 | tf_op jit(solution)/shard_map/dot_general | solution.py:90
  61.7 30.6 %all_gather.34 = bf16[16,4096]{1,0:T(8,128)(2,1)S(1)} all-gather(bf16[16,512]{1,0:T(8,128)(2,1)S(1)} %fusion.12), channel_id=1, replica_groups=mesh['grp'=2,'tp'=8,'sub'=2] {'tp'}, dimensions={1}, use_global_device_ids=true | all-gather | bytes 147456 | tf_op jit(solution)/shard_map/all_gather | solution.py:100
  92.5 0.3 fusion.48
  92.8 1.3 fusion.26
  94.2 9.4 %copy.83 = bf16[512,8,2,512]{3,1,2,0:T(8,128)(2,1)} copy(bf16[512,8,2,512]{3,2,1,0:T(2,128)(2,1)} %bitcast.89) | data formatting | bytes 16777216
  103.6 12.0 %copy.75 = bf16[1024,4096]{1,0:T(8,128)(2,1)} copy(bf16[1024,4096]{0,1:T(8,128)(2,1)} %bitcast.88) | data formatting | bytes 16777216 | tf_op jit(solution)/shard_map/dot_general | solution.py:144
  115.7 0.4 fusion.15
  116.1 31.1 %all-gather.3 = bf16[8,64,16]{1,2,0:T(8,128)(2,1)S(1)} all-gather(bf16[1,64,16]{1,2,0:T(8,128)(2,1)S(1)} %fusion.15), channel_id=1, replica_groups=mesh['grp'=2,'tp'=8,'sub'=2] {'tp'}, dimensions={0}, use_global_device_ids=true | all-gather | bytes 18432 | tf_op jit(solution)/shard_map/all_gather | solution.py:101
  147.4 0.3 multiply_reduce_fusion
  147.9 30.9 %all-gather.1 = f32[128,4,8]{2,1,0:T(4,128)S(1)} all-gather(f32[16,4,8]{2,1,0:T(4,128)S(1)} %fusion.27), channel_id=3, replica_groups=mesh['grp'=2,'tp'=8,'sub'=2] {'tp'}, dimensions={0}, use_global_device_ids=true | all-gather | bytes 18432 | tf_op jit(solution)/shard_map/all_gather | solution.py:14
  179.0 30.7 %all-gather = f32[128,4,8]{2,1,0:T(4,128)S(1)} all-gather(f32[16,4,8]{2,1,0:T(4,128)S(1)} %get-tuple-element.236), channel_id=2, replica_groups=mesh['grp'=2,'tp'=8,'sub'=2] {'tp'}, dimensions={0}, use_global_device_ids=true | all-gather | bytes 18432 | tf_op jit(solution)/shard_map/all_gather | solution.py:14
  210.0 0.4 fusion.16
  210.4 30.6 %all-gather.4 = bf16[8,64,16]{1,2,0:T(8,128)(2,1)S(1)} all-gather(bf16[1,64,16]{1,2,0:T(8,128)(2,1)S(1)} %fusion.16), channel_id=1, replica_groups=mesh['grp'=2,'tp'=8,'sub'=2] {'tp'}, dimensions={0}, use_global_device_ids=true | all-gather | bytes 18432 | tf_op jit(solution)/shard_map/all_gather | solution.py:102
  241.1 1.0 slice.26
  242.1 10.0 %while.19 = (s32[]{:T(128)}, f32[16,4,8]{0,2,1:T(8,128)S(1)}, f32[16,4,8]{0,2,1:T(8,128)S(1)}, f32[16,4,8,128]{3,2,1,0:T(8,128)S(1)}, f32[8,16,4,8]{1,3,2,0:T(8,...) while((s32[]{:T(128)}, f32[16,4,8]{0,2,1:T(8,128)S(1)}, ...), condition=%wide.region_4.5_spmd, body=%wide.region_3.4_spmd.sunk | while | flops 199685 | bytes 815255 | solution.py:19
  242.3 1.2 fusion.58
  243.7 1.2 fusion.58
  245.2 1.2 fusion.58
  246.6 1.2 fusion.58
  248.0 1.2 fusion.58
  249.4 1.2 fusion.58
  250.9 1.2 fusion.58
  252.3 0.3 divide_convert_fusion
  252.7 6.3 %fusion.49 = f32[16,2,512]{2,0,1:T(8,128)} fusion(bf16[16,4096,1]{1,0,2:T(8,128)(2,1)S(1)} %reshape.198, bf16[2,512,4096]{2,1,0:T(8,128)(2,1)} %bitcast.87), kind=kOutput, calls=%fused_computation.94 | convolution fusion | flops 134217728 | bytes 8585216 | tf_op jit(solution)/shard_map/dot_general | solution.py:144
  259.1 4.8 %reduce-scatter.2.cloned.1.call-done = f32[16,1,512]{2,0,1:T(8,128)} async-done(((f32[16,2,512]{2,0,1:T(8,128)}), f32[16,1,512]{2,0,1:T(8,128)}) %reduce-scatter.2.cloned.1.call-update) | async-done | bytes 32784 | tf_op jit(solution)/shard_map/reduce_scatter | solution.py:148
  263.9 0.8 add_convert_fusion.1
  264.7 30.8 %all_gather.43 = bf16[16,1,4096]{2,0,1:T(8,128)(2,1)S(1)} all-gather(bf16[16,1,512]{2,0,1:T(8,128)(2,1)S(1)} %add_convert_fusion.1), channel_id=1, replica_groups=mesh['grp'=2,'tp'=8,'sub'=2] {'tp'}, dimensions={2}, use_global_device_ids=true | all-gather | bytes 147456 | tf_op jit(solution)/shard_map/all_gather | solution.py:49
  295.6 2.6 psum.28
  298.3 7.9 %fusion.7 = f32[16,1792]{1,0:T(8,128)} fusion(bf16[1,4096,1792]{2,1,0:T(8,128)(2,1)} %param.22, bf16[16,1,4096]{2,0,1:T(8,128)(2,1)S(1)} %all_gather.43, f32[4096]{0:T(1024)S(1)} %dynamic_slice.55, f32[16]{0:T(128)S(1)} %add_rsqrt_fusion), kind=kOutput, calls=%fused_computation.12 | convolution fusion | flops 235143168 | bytes 14942272 | tf_op jit(solution)/shard_map/dot_general | solution.py:158
  306.1 8.0 %fusion.5 = f32[16,1792]{1,0:T(8,128)} fusion(bf16[1,4096,1792]{2,1,0:T(8,128)(2,1)} %param.23, bf16[16,1,4096]{2,0,1:T(8,128)(2,1)S(1)} %all_gather.43, f32[4096]{0:T(1024)S(1)} %dynamic_slice.55, f32[16]{0:T(128)S(1)} %add_rsqrt_fusion), kind=kOutput, calls=%fused_computation.10 | convolution fusion | flops 235143168 | bytes 14942272 | tf_op jit(solution)/shard_map/dot_general | solution.py:161
  314.2 19.1 %all-reduce.6.cloned.1.call-done = (f32[16,1792]{1,0:T(8,128)}, f32[16,1792]{1,0:T(8,128)}) async-done(((f32[16,1792]{1,0:T(8,128)}, f32[16,1792]{1,0:T(8,128)}), (f32[16,1792]{1,0:T(8,128)}, f32[16,1792]{1,0:T(8,128)})) %all-reduce.6.cloned.1.call-update) | async-done | bytes 229392 | tf_op jit(solution)/shard_map/psum | solution.py:162
  333.3 8.0 %fusion.3 = f32[16,4096]{1,0:T(8,128)} fusion(bf16[1792,1,4096]{2,0,1:T(8,128)(2,1)} %param.24, f32[16,1792]{1,0:T(8,128)} %get-tuple-element.221, f32[16,1792]{1,0:T(8,128)} %get-tuple-element.222), kind=kOutput, calls=%fused_computation.8 | convolution fusion | flops 235053056 | bytes 15171584 | tf_op jit(solution)/shard_map/dot_general | solution.py:164
  341.4 72.4 %all-reduce.4.cloned.1.call-done = f32[16,4096]{1,0:T(8,128)} async-done(((f32[16,4096]{1,0:T(8,128)}), f32[16,4096]{1,0:T(8,128)}) %all-reduce.4.cloned.1.call-update) | async-done | bytes 262160 | tf_op jit(solution)/shard_map/psum | solution.py:167
  413.8 1.4 fusion.37
  (99 shorter events, 3.8 us)
Async XLA Ops:
  6.5 109.1 %copy-start = (bf16[8192,1,64]{0,2,1:T(8,128)(2,1)S(1)}, bf16[8192,1,64]{0,2,1:T(8,128)(2,1)}, u32[]{:S(2)}) copy-start(bf16[8192,1,64]{0,2,1:T(8,128)(2,1)} %param.18) | copy-start | bytes 3145732
  6.5 85.9 %copy-start.4 = (bf16[16,8,4,128]{3,2,1,0:T(4,128)(2,1)S(1)}, bf16[16,8,4,128]{3,2,1,0:T(4,128)(2,1)}, u32[]{:S(2)}) copy-start(bf16[16,8,4,128]{3,2,1,0:T(4,128)(2,1)} %param.25) | copy-start | bytes 393220
  6.5 86.3 %copy-start.5 = (bf16[16,8,4,128]{3,2,1,0:T(4,128)(2,1)S(1)}, bf16[16,8,4,128]{3,2,1,0:T(4,128)(2,1)}, u32[]{:S(2)}) copy-start(bf16[16,8,4,128]{3,2,1,0:T(4,128)(2,1)} %param.26) | copy-start | bytes 393220
  6.5 234.6 %all-gather.7.cloned.1.call-start = ((), (), s32[]{:S(2)}) async-start(), calls=%async_computation.3 | async-start | bytes 2359296 | tf_op jit(solution)/shard_map/all_gather | solution.py:14
  6.5 8.0 %collective-permute-start = (bf16[16,1,512]{2,0,1:T(8,128)(2,1)}, bf16[16,1,512]{2,0,1:T(8,128)(2,1)S(1)}, u32[]{:S(2)}, u32[]{:S(2)}) collective-permute-start(bf16[16,1,512]{2,0,1:T(8,128)(2,1)} %param.15), channel_id=1, source_target_pairs={{0,2},{2,4},{4,6},{6,8},{8,10},{10,12},{12,14},{14,0},{1,3},{3,5},... | collective-permute-start | bytes 49160 | tf_op jit(solution)/shard_map/ppermute | solution.py:41
  14.5 6.4 %collective-permute-start.1 = (bf16[16,1,512]{2,0,1:T(8,128)(2,1)S(1)}, bf16[16,1,512]{2,0,1:T(8,128)(2,1)S(1)}, u32[]{:S(2)}, u32[]{:S(2)}) collective-permute-start(bf16[16,1,512]{2,0,1:T(8,128)(2,1)S(1)} %collective-permute-done), channel_id=1, source_target_pairs={{0,2},{2,4},{4,6},{6,8},{8,10},{10,12},{12,14},{14,0},{1,3},{3,5},... | collective-permute-start | bytes 49160 | tf_op jit(solution)/shard_map/ppermute | solution.py:41
  21.0 6.4 %collective-permute-start.2 = (bf16[16,1,512]{2,0,1:T(8,128)(2,1)S(1)}, bf16[16,1,512]{2,0,1:T(8,128)(2,1)S(1)}, u32[]{:S(2)}, u32[]{:S(2)}) collective-permute-start(bf16[16,1,512]{2,0,1:T(8,128)(2,1)S(1)} %collective-permute-done.1), channel_id=1, source_target_pairs={{0,2},{2,4},{4,6},{6,8},{8,10},{10,12},{12,14},{14,0},{1,3},{3,5},... | collective-permute-start | bytes 49160 | tf_op jit(solution)/shard_map/ppermute | solution.py:41
  27.4 6.4 %collective-permute-start.3 = (bf16[16,1,512]{2,0,1:T(8,128)(2,1)S(1)}, bf16[16,1,512]{2,0,1:T(8,128)(2,1)S(1)}, u32[]{:S(2)}, u32[]{:S(2)}) collective-permute-start(bf16[16,1,512]{2,0,1:T(8,128)(2,1)S(1)} %collective-permute-done.2), channel_id=1, source_target_pairs={{0,2},{2,4},{4,6},{6,8},{8,10},{10,12},{12,14},{14,0},{1,3},{3,5},... | collective-permute-start | bytes 49160 | tf_op jit(solution)/shard_map/ppermute | solution.py:41
  33.8 6.4 %collective-permute-start.4 = (bf16[16,1,512]{2,0,1:T(8,128)(2,1)S(1)}, bf16[16,1,512]{2,0,1:T(8,128)(2,1)S(1)}, u32[]{:S(2)}, u32[]{:S(2)}) collective-permute-start(bf16[16,1,512]{2,0,1:T(8,128)(2,1)S(1)} %collective-permute-done.3), channel_id=1, source_target_pairs={{0,2},{2,4},{4,6},{6,8},{8,10},{10,12},{12,14},{14,0},{1,3},{3,5},... | collective-permute-start | bytes 49160 | tf_op jit(solution)/shard_map/ppermute | solution.py:41
  40.3 6.4 %collective-permute-start.5 = (bf16[16,1,512]{2,0,1:T(8,128)(2,1)S(1)}, bf16[16,1,512]{2,0,1:T(8,128)(2,1)S(1)}, u32[]{:S(2)}, u32[]{:S(2)}) collective-permute-start(bf16[16,1,512]{2,0,1:T(8,128)(2,1)S(1)} %collective-permute-done.4), channel_id=1, source_target_pairs={{0,2},{2,4},{4,6},{6,8},{8,10},{10,12},{12,14},{14,0},{1,3},{3,5},... | collective-permute-start | bytes 49160 | tf_op jit(solution)/shard_map/ppermute | solution.py:41
  46.7 6.4 %collective-permute-start.6 = (bf16[16,1,512]{2,0,1:T(8,128)(2,1)S(1)}, bf16[16,1,512]{2,0,1:T(8,128)(2,1)S(1)}, u32[]{:S(2)}, u32[]{:S(2)}) collective-permute-start(bf16[16,1,512]{2,0,1:T(8,128)(2,1)S(1)} %collective-permute-done.5), channel_id=1, source_target_pairs={{0,2},{2,4},{4,6},{6,8},{8,10},{10,12},{12,14},{14,0},{1,3},{3,5},... | collective-permute-start | bytes 49160 | tf_op jit(solution)/shard_map/ppermute | solution.py:41
  94.1 169.8 %reduce-scatter.2.cloned.1.call-start = ((), (), s32[]{:S(2)}) async-start(), calls=%async_computation.1 | async-start | bytes 98304 | tf_op jit(solution)/shard_map/reduce_scatter | solution.py:148
  94.2 115.8 %copy-start.2 = (bf16[8192,1,64]{0,2,1:T(8,128)(2,1)S(1)}, bf16[8192,1,64]{0,2,1:T(8,128)(2,1)}, u32[]{:S(2)}) copy-start(bf16[8192,1,64]{0,2,1:T(8,128)(2,1)} %param.19) | copy-start | bytes 3145732
  115.7 143.4 %copy-start.6 = (f32[8192]{0:T(1024)S(1)}, f32[8192]{0:T(1024)}, u32[]{:S(2)}) copy-start(f32[8192]{0:T(1024)} %param.21) | copy-start | bytes 98308
  115.7 148.3 %copy-start.3 = (bf16[16,1,512]{2,0,1:T(8,128)(2,1)S(1)}, bf16[16,1,512]{2,0,1:T(8,128)(2,1)}, u32[]{:S(2)}) copy-start(bf16[16,1,512]{2,0,1:T(8,128)(2,1)} %param.15) | copy-start | bytes 49156
  259.0 74.3 %all-reduce.6.cloned.1.call-start = ((), (), s32[]{:S(2)}) async-start(), calls=%async_computation.4 | async-start | bytes 458752 | tf_op jit(solution)/shard_map/psum | solution.py:162
  306.1 109.0 %copy-start.1 = (bf16[8192,1,64]{0,2,1:T(8,128)(2,1)S(1)}, bf16[8192,1,64]{0,2,1:T(8,128)(2,1)}, u32[]{:S(2)}) copy-start(bf16[8192,1,64]{0,2,1:T(8,128)(2,1)} %param.18) | copy-start | bytes 3145732
  314.1 99.6 %all-reduce.4.cloned.1.call-start = ((), (), s32[]{:S(2)}) async-start(), calls=%async_computation.2 | async-start | bytes 524288 | tf_op jit(solution)/shard_map/psum | solution.py:167
Sparse Core Ops, SparseCore 0:
  94.3 47.1 all-gather.6
  259.1 4.7 reduce-scatter.1
  314.2 19.0 all-reduce.5
  341.5 72.2 all-reduce.3
